TPU v7x, 32 devices: a whole 2x2x4 slice. The times are simulated.
32 devices in a mesh: layer: 8 (over y, x, core), latent: 4 (over z).
Axes of the slice: x: 2, y: 2, z: 4, core: 2. Of those that a mesh axis runs over, the one named last changes fastest.
Arguments:
- decoder: bfloat16 [65536, 4, 2304], P(('layer', 'latent')), may hold values from -0.375 to 0.375
- code_index: int32 [4, 128, 64], replicated, may hold values from 0 to 16383, all different within a row
- code_value: bfloat16 [4, 128, 64], replicated, may hold values from 0.19921875 to 4
- bias: float32 [4, 2304], replicated, may hold values from -3 to 3
- target: bfloat16 [4, 128, 2304], replicated, may hold values from -6 to 6
Outputs:
- layer_error: float32 [4], replicated
- grad_decoder: bfloat16 [65536, 4, 2304], P(('layer', 'latent'))
- code_grad: float32 [4, 128, 64], replicated
Inputs may be any that keep to these rules, and one draw needn't show every extreme that they name: `code_index`: the 64 indices of one token in one layer are distinct.
All inputs are finite; a program needn't handle non-finite values.
Results may differ from a plain program's by a relative error of at most 0.0048.
Values may be sent and summed in bfloat16 or wider, within the bound.
No kernel may reach another device: no remote copies, remote signals or barrier semaphores. Data moves between devices by JAX's collectives and lax.ppermute only.
A program may use at most 192 MiB of HBM per device.

v0:
```python
import jax
import jax.numpy as jnp
from jax import lax
from jax.sharding import PartitionSpec as P

D = 2304
LAYERS = 4
TOPK = 64
TOKENS = 128


def build_codes(index_rows, value_rows, offset, slab_width):
    columns = offset + lax.iota(jnp.int32, slab_width)
    matches = index_rows[:, :, None] == columns[None, None, :]
    dense = jnp.sum(jnp.where(matches, value_rows[:, :, None].astype(jnp.float32), 0.0), axis=1)
    return (matches, dense.astype(jnp.bfloat16))


def contract_rows(left, right):
    return lax.dot_general(
        left, right, (((0,), (0,)), ((), ())), preferred_element_type=jnp.float32
    )


def contract_cols(left, right):
    return lax.dot_general(
        left, right, (((1,), (1,)), ((), ())), preferred_element_type=jnp.float32
    )


def on_device(decoder, code_index, code_value, bias, target):
    layer_count = lax.axis_size("layer")
    latent_count = lax.axis_size("latent")
    group_size = layer_count // LAYERS
    slab_width = decoder.shape[0]
    layer_pos = lax.axis_index("layer")
    source = layer_pos // group_size
    offset = (layer_pos % group_size * latent_count + lax.axis_index("latent")) * slab_width
    matches, dense_codes = build_codes(
        lax.dynamic_index_in_dim(code_index, source, 0, keepdims=False),
        lax.dynamic_index_in_dim(code_value, source, 0, keepdims=False),
        offset,
        slab_width,
    )

    def forward_step(target_layer, totals):
        weight_slab = lax.dynamic_index_in_dim(decoder, target_layer, 1, keepdims=False)
        product = jnp.dot(dense_codes, weight_slab, preferred_element_type=jnp.float32)
        return lax.dynamic_update_index_in_dim(totals, product, target_layer, 0)

    partials = jnp.zeros((LAYERS, TOKENS, D), jnp.float32)
    stop_at = LAYERS
    partials = lax.fori_loop(source, stop_at, forward_step, partials)
    recon_sum = lax.psum(partials, ("layer", "latent"))
    residual = recon_sum + bias[:, None, :] - target.astype(jnp.float32)
    layer_error = jnp.mean(residual * residual, axis=(1, 2))
    error_b = residual.astype(jnp.bfloat16)

    def backward_step(target_layer, state_pair):
        grads, code_sums = state_pair
        weight_slab = lax.dynamic_index_in_dim(decoder, target_layer, 1, keepdims=False)
        target_error = lax.dynamic_index_in_dim(error_b, target_layer, 0, keepdims=False)
        grad_block = contract_rows(dense_codes, target_error).astype(jnp.bfloat16)
        grads = lax.dynamic_update_index_in_dim(grads, grad_block, target_layer, 1)
        return (grads, code_sums + contract_cols(target_error, weight_slab))

    start_pair = (
        jnp.zeros(decoder.shape, jnp.bfloat16),
        jnp.zeros((TOKENS, slab_width), jnp.float32),
    )
    grads, code_sums = lax.fori_loop(source, stop_at, backward_step, start_pair)
    picked = jnp.sum(jnp.where(matches, code_sums[:, None, :], 0.0), axis=2)
    code_parts = lax.dynamic_update_index_in_dim(
        jnp.zeros((LAYERS, TOKENS, TOPK), jnp.float32), picked, source, 0
    )
    code_grad = lax.psum(code_parts, ("layer", "latent"))
    return (layer_error, grads, code_grad)


def solution(mesh):
    placed = (P(("layer", "latent"), None, None), P(), P(), P(), P())
    return jax.shard_map(
        on_device,
        mesh=mesh,
        in_specs=placed,
        out_specs=(P(), P(("layer", "latent"), None, None), P()),
        check_vma=False,
    )
```

profile of v0, /device:TPU:0, one launch (start us, length us, event | category | flops | bytes accessed | tf_op | source)
XLA Modules:
  0.0 428.5 jit_solution(2103701920801345203)
XLA Ops:
  7.2 25.9 %copy.19 = bf16[2048,4,2304]{2,0,1:T(8,128)(2,1)} copy(bf16[2048,4,2304]{2,1,0:T(4,128)(2,1)} %param.9) | data formatting | bytes 75497472 | tf_op jit(solution)/shard_map/while | solution.py:53
  33.1 0.7 bitcast_convert_fusion
  34.1 9.8 %fusion.21 = bf16[128,2048]{1,0:T(8,128)(2,1)S(1)} fusion(f32[128,64]{1,0:T(8,128)S(1)} %copy.18, s32[2048]{0:T(1024)S(1)} %iota_add_fusion, s32[128,64]{1,0:T(8,128)S(1)} %copy.17), kind=kLoop, calls=%fused_computation.21 | loop fusion | flops 50069504 | bytes 598016 | tf_op jit(solution)/shard_map/reduce_sum | solution.py:15
  43.9 2.6 broadcast_in_dim.51.clone
  46.5 26.9 %while.22 = (s32[]{:T(128)}, f32[4,128,2304]{2,1,0:T(8,128)}, bf16[2048,4,2304]{2,0,1:T(8,128)(2,1)}, bf16[128,2048]{1,0:T(8,128)(2,1)S(1)}, s32[]{:T(128)}, /*index=5*/s32[]{:T(128)}, s32[]{:T(128)}) while((s32[]{:T(128)}, f32[4,128,2304]{2,1,0:T(8,128)}, bf16[2048,4,2304]{2,0,1:T(8,128)(2,1)}, bf16[128,2048]{1,0:T(8,128)(2,1)S(1)}, ...), condition=%wide.region_2.3_spmd, body=%wide.region_1.2_spmd.sunk | while | flops 1207959552 | bytes 15859839 | solution.py:53
  46.5 5.2 %fusion.37 = f32[1,128,2304]{1,2,0:T(8,128)S(1)} fusion(bf16[128,2048]{1,0:T(8,128)(2,1)S(1)} %get-tuple-element.191, bf16[2048,4,2304]{2,0,1:T(8,128)(2,1)} %get-tuple-element.190, s32[]{:T(128)S(6)} %select_n.53), kind=kOutput, calls=%fused_computation.3.clone.1 | convolution fusion | flops 1207959552 | bytes 11141124 | tf_op jit(solution)/shard_map/while/body/dot_general | solution.py:48
  51.7 0.4 copy.30
  52.1 1.1 constant_dynamic-update-slice_fusion.3
  53.2 5.2 %fusion.37 = f32[1,128,2304]{1,2,0:T(8,128)S(1)} fusion(bf16[128,2048]{1,0:T(8,128)(2,1)S(1)} %get-tuple-element.191, bf16[2048,4,2304]{2,0,1:T(8,128)(2,1)} %get-tuple-element.190, s32[]{:T(128)S(6)} %select_n.53), kind=kOutput, calls=%fused_computation.3.clone.1 | convolution fusion | flops 1207959552 | bytes 11141124 | tf_op jit(solution)/shard_map/while/body/dot_general | solution.py:48
  58.8 1.1 constant_dynamic-update-slice_fusion.3
  59.9 5.2 %fusion.37 = f32[1,128,2304]{1,2,0:T(8,128)S(1)} fusion(bf16[128,2048]{1,0:T(8,128)(2,1)S(1)} %get-tuple-element.191, bf16[2048,4,2304]{2,0,1:T(8,128)(2,1)} %get-tuple-element.190, s32[]{:T(128)S(6)} %select_n.53), kind=kOutput, calls=%fused_computation.3.clone.1 | convolution fusion | flops 1207959552 | bytes 11141124 | tf_op jit(solution)/shard_map/while/body/dot_general | solution.py:48
  65.5 1.1 constant_dynamic-update-slice_fusion.3
  66.6 5.2 %fusion.37 = f32[1,128,2304]{1,2,0:T(8,128)S(1)} fusion(bf16[128,2048]{1,0:T(8,128)(2,1)S(1)} %get-tuple-element.191, bf16[2048,4,2304]{2,0,1:T(8,128)(2,1)} %get-tuple-element.190, s32[]{:T(128)S(6)} %select_n.53), kind=kOutput, calls=%fused_computation.3.clone.1 | convolution fusion | flops 1207959552 | bytes 11141124 | tf_op jit(solution)/shard_map/while/body/dot_general | solution.py:48
  72.2 1.2 constant_dynamic-update-slice_fusion.3
  73.5 145.7 %all-reduce.3.cloned.1.call-done = f32[4,128,2304]{2,1,0:T(8,128)} async-done(((f32[4,128,2304]{2,1,0:T(8,128)}), f32[4,128,2304]{2,1,0:T(8,128)}) %all-reduce.3.cloned.1.call-update) | async-done | bytes 4718608 | tf_op jit(solution)/shard_map/psum | solution.py:54
  219.2 4.1 fusion.23
  223.3 12.5 %broadcast_in_dim.54 = bf16[2048,4,2304]{0,2,1:T(8,128)(2,1)} broadcast(bf16[]{:T(256)} %constant.88.clone.1), dimensions={} | broadcast | bytes 37748736 | tf_op jit(solution)/shard_map/broadcast_in_dim | solution.py:68
  235.9 52.3 %while.23 = (s32[]{:T(128)}, bf16[2048,4,2304]{0,2,1:T(8,128)(2,1)}, f32[128,2048]{1,0:T(8,128)S(1)}, bf16[4,128,2304]{2,1,0:T(8,128)(2,1)S(1)}, bf16[128,2048]{...) while((s32[]{:T(128)}, bf16[2048,4,2304]{0,2,1:T(8,128)(2,1)}, ...), condition=%wide.region_6.7_spmd, body=%wide.region_5.6_spmd.sunk | while | flops 2420899840 | bytes 22677640 | solution.py:71
  236.0 6.1 %fusion.42 = bf16[2048,4,2304]{0,2,1:T(8,128)(2,1)} fusion(bf16[2048,4,2304]{0,2,1:T(8,128)(2,1)} %get-tuple-element.205, s32[]{:T(128)S(6)} %select_n.54, bf16[128,2048]{1,0:T(8,128)(2,1)} %get-tuple-element.217, bf16[4,128,2304]{2,1,0:T(8,128)(2,1)S(1)} %get-tuple-element.216), kind=kOutput, calls=%fused_computation.8.clone.1 | convolution fusion | flops 1212678144 | bytes 10552320 | tf_op jit(solution)/shard_map/while/body/dot_general | solution.py:20
  242.1 6.9 %fusion.43 = f32[128,2048]{1,0:T(8,128)S(1)} fusion(f32[128,2048]{1,0:T(8,128)S(1)} %get-tuple-element.206, bf16[2048,4,2304]{2,0,1:T(8,128)(2,1)} %get-tuple-element.218, s32[]{:T(128)S(6)} %select_n.54, bf16[4,128,2304]{2,1,0:T(8,128)(2,1)S(1)} %get-tuple-element.216), kind=kOutput, calls=%fused_computation.12.clone.1 | convolution fusion | flops 1208221696 | bytes 12125184 | tf_op jit(solution)/shard_map/while/body/dot_general | solution.py:26
  249.0 6.1 %fusion.42 = bf16[2048,4,2304]{0,2,1:T(8,128)(2,1)} fusion(bf16[2048,4,2304]{0,2,1:T(8,128)(2,1)} %get-tuple-element.205, s32[]{:T(128)S(6)} %select_n.54, bf16[128,2048]{1,0:T(8,128)(2,1)} %get-tuple-element.217, bf16[4,128,2304]{2,1,0:T(8,128)(2,1)S(1)} %get-tuple-element.216), kind=kOutput, calls=%fused_computation.8.clone.1 | convolution fusion | flops 1212678144 | bytes 10552320 | tf_op jit(solution)/shard_map/while/body/dot_general | solution.py:20
  255.1 6.9 %fusion.43 = f32[128,2048]{1,0:T(8,128)S(1)} fusion(f32[128,2048]{1,0:T(8,128)S(1)} %get-tuple-element.206, bf16[2048,4,2304]{2,0,1:T(8,128)(2,1)} %get-tuple-element.218, s32[]{:T(128)S(6)} %select_n.54, bf16[4,128,2304]{2,1,0:T(8,128)(2,1)S(1)} %get-tuple-element.216), kind=kOutput, calls=%fused_computation.12.clone.1 | convolution fusion | flops 1208221696 | bytes 12125184 | tf_op jit(solution)/shard_map/while/body/dot_general | solution.py:26
  262.1 6.2 %fusion.42 = bf16[2048,4,2304]{0,2,1:T(8,128)(2,1)} fusion(bf16[2048,4,2304]{0,2,1:T(8,128)(2,1)} %get-tuple-element.205, s32[]{:T(128)S(6)} %select_n.54, bf16[128,2048]{1,0:T(8,128)(2,1)} %get-tuple-element.217, bf16[4,128,2304]{2,1,0:T(8,128)(2,1)S(1)} %get-tuple-element.216), kind=kOutput, calls=%fused_computation.8.clone.1 | convolution fusion | flops 1212678144 | bytes 10552320 | tf_op jit(solution)/shard_map/while/body/dot_general | solution.py:20
  268.3 6.9 %fusion.43 = f32[128,2048]{1,0:T(8,128)S(1)} fusion(f32[128,2048]{1,0:T(8,128)S(1)} %get-tuple-element.206, bf16[2048,4,2304]{2,0,1:T(8,128)(2,1)} %get-tuple-element.218, s32[]{:T(128)S(6)} %select_n.54, bf16[4,128,2304]{2,1,0:T(8,128)(2,1)S(1)} %get-tuple-element.216), kind=kOutput, calls=%fused_computation.12.clone.1 | convolution fusion | flops 1208221696 | bytes 12125184 | tf_op jit(solution)/shard_map/while/body/dot_general | solution.py:26
  275.2 6.1 %fusion.42 = bf16[2048,4,2304]{0,2,1:T(8,128)(2,1)} fusion(bf16[2048,4,2304]{0,2,1:T(8,128)(2,1)} %get-tuple-element.205, s32[]{:T(128)S(6)} %select_n.54, bf16[128,2048]{1,0:T(8,128)(2,1)} %get-tuple-element.217, bf16[4,128,2304]{2,1,0:T(8,128)(2,1)S(1)} %get-tuple-element.216), kind=kOutput, calls=%fused_computation.8.clone.1 | convolution fusion | flops 1212678144 | bytes 10552320 | tf_op jit(solution)/shard_map/while/body/dot_general | solution.py:20
  281.3 6.9 %fusion.43 = f32[128,2048]{1,0:T(8,128)S(1)} fusion(f32[128,2048]{1,0:T(8,128)S(1)} %get-tuple-element.206, bf16[2048,4,2304]{2,0,1:T(8,128)(2,1)} %get-tuple-element.218, s32[]{:T(128)S(6)} %select_n.54, bf16[4,128,2304]{2,1,0:T(8,128)(2,1)S(1)} %get-tuple-element.216), kind=kOutput, calls=%fused_computation.12.clone.1 | convolution fusion | flops 1208221696 | bytes 12125184 | tf_op jit(solution)/shard_map/while/body/dot_general | solution.py:26
  288.2 9.0 %fusion.22 = f32[128,64]{1,0:T(8,128)S(1)} fusion(f32[128,2048]{1,0:T(8,128)S(1)} %get-tuple-element.60, s32[2048]{0:T(1024)S(1)} %iota_add_fusion, s32[128,64]{1,0:T(8,128)S(1)} %copy.17), kind=kLoop, calls=%fused_computation.22 | loop fusion | flops 50323456 | bytes 1122304 | tf_op jit(solution)/shard_map/reduce_sum | solution.py:72
  297.4 0.6 copy-done.3
  298.0 0.5 broadcast_multiply_fusion
  298.6 57.6 %copy.23 = bf16[2048,4,2304]{2,1,0:T(4,128)(2,1)} copy(bf16[2048,4,2304]{0,2,1:T(8,128)(2,1)} %get-tuple-element.88) | data formatting | bytes 75497472
  356.2 63.9 %all-reduce.5.cloned.1.call-done = f32[4,128,64]{1,2,0:T(8,128)} async-done(((f32[4,128,64]{1,2,0:T(8,128)}), f32[4,128,64]{1,2,0:T(8,128)}) %all-reduce.5.cloned.1.call-update) | async-done | bytes 131088 | tf_op jit(solution)/shard_map/psum | solution.py:76
  420.1 1.6 copy.51
  (24 shorter events, 1.6 us)
Async XLA Ops:
  7.2 26.8 %copy-start = (s32[4,128,64]{1,2,0:T(8,128)S(1)}, s32[4,128,64]{1,2,0:T(8,128)}, u32[]{:S(2)}) copy-start(s32[4,128,64]{1,2,0:T(8,128)} %param.10) | copy-start | bytes 393220
  7.2 212.0 %all-reduce.3.cloned.1.call-start = ((), (), s32[]{:S(2)}) async-start(), calls=%async_computation | async-start | bytes 9437184 | tf_op jit(solution)/shard_map/psum | solution.py:54
  46.5 172.7 %copy-start.4 = (f32[4,2304]{1,0:T(4,128)S(1)}, f32[4,2304]{1,0:T(4,128)}, u32[]{:S(2)}) copy-start(f32[4,2304]{1,0:T(4,128)} %param.12) | copy-start | bytes 110596
  73.4 149.9 %copy-start.2 = (bf16[128,2048]{1,0:T(8,128)(2,1)}, bf16[128,2048]{1,0:T(8,128)(2,1)S(1)}, u32[]{:S(2)}) copy-start(bf16[128,2048]{1,0:T(8,128)(2,1)S(1)} %get-tuple-element.230) | copy-start | bytes 1572868
  73.4 346.6 %all-reduce.5.cloned.1.call-start = ((), (), s32[]{:S(2)}) async-start(), calls=%async_computation.1 | async-start | bytes 262144 | tf_op jit(solution)/shard_map/psum | solution.py:76
  297.4 0.7 copy-start.3
  298.6 123.1 %copy-start.1 = (s32[4,128,64]{1,2,0:T(8,128)S(1)}, s32[4,128,64]{1,2,0:T(8,128)}, u32[]{:S(2)}) copy-start(s32[4,128,64]{1,2,0:T(8,128)} %param.10) | copy-start | bytes 393220
Sparse Core Ops, SparseCore 0:
  73.5 145.6 all-reduce.2
  298.2 121.8 all-reduce.4
where the time goes:
time: 430 us; the launch traced here: 428 us
  waiting for transfers between devices  210 us (49%)
  local copies, waits for them, and re-layouts  107 us (25%)
  matrix products  73 us (17%)
  other arithmetic  24.2 us (6%)
  between operations  14.2 us (3%)
    psum x1, waiting for transfers between devices, on_device(): recon_sum = lax.psum(partials, ('layer', 'latent'))  146 us
    psum x1, waiting for transfers between devices, on_device(): code_grad = lax.psum(code_parts, ('layer', 'latent'))  63.9 us
    unnamed x12, local copies, waits for them, and re-layouts  59.9 us
    dot_general x4, matrix products, contract_cols(): lax.dot_general(left, right, (((1,), (1,)), ((), ())), preferred_element_...  27.6 us
    while x1, local copies, waits for them, and re-layouts, on_device(): partials = lax.fori_loop(source, stop_at, forward_step, partials)  25.9 us
    dot_general x4, matrix products, contract_rows(): lax.dot_general(left, right, (((0,), (0,)), ((), ())), preferred_element_...  24.6 us
    dot_general x4, matrix products, forward_step(): jnp.dot(dense_codes, weight_slab, preferred_element_type=jnp.float32)  20.9 us
    broadcast_in_dim x1, local copies, waits for them, and re-layouts, on_device(): jnp.zeros(decoder.shape, jnp.bfloat16)  12.5 us
  transfers between devices with their start and end apart: 2, of which 2 were waited for; matrix products, arithmetic and copies ran while one was open for 14% of the time, Pallas kernels for 0%

commit v1 on v0

--- a/solution.py
+++ b/solution.py
@@ -7,6 +7,10 @@
 LAYERS = 4
 TOPK = 64
 TOKENS = 128
+
+
+def see_positions(q_in):
+    return lax.psum(lax.psum(q_in, "latent"), "layer")
 
 
 def build_codes(index_rows, value_rows, offset, slab_width):
@@ -51,7 +55,7 @@
     partials = jnp.zeros((LAYERS, TOKENS, D), jnp.float32)
     stop_at = LAYERS
     partials = lax.fori_loop(source, stop_at, forward_step, partials)
-    recon_sum = lax.psum(partials, ("layer", "latent"))
+    recon_sum = see_positions(partials)
     residual = recon_sum + bias[:, None, :] - target.astype(jnp.float32)
     layer_error = jnp.mean(residual * residual, axis=(1, 2))
     error_b = residual.astype(jnp.bfloat16)

time: 430 us -> 548 us (1.27)
  waiting for transfers between devices: 210 us -> 327 us
    psum x1 -> x2, waiting for transfers between devices: 146 us -> 262 us  [see_positions(): return lax.psum(lax.psum(q_in, 'latent'), 'layer')]
  transfers between devices with their start and end apart: 2 -> 3, of which waited for: 2 -> 3; matrix products, arithmetic and copies ran while one was open for 14% -> 11% of each run, Pallas kernels for 0% -> 0%
where the time goes in v1:
time: 548 us; the launch traced here: 546 us
  waiting for transfers between devices  327 us (60%)
  local copies, waits for them, and re-layouts  107 us (20%)
  matrix products  73 us (13%)
  other arithmetic  24.2 us (4%)
  between operations  13.9 us (3%)
    psum x2, waiting for transfers between devices, see_positions(): return lax.psum(lax.psum(q_in, 'latent'), 'layer')  262 us
    psum x1, waiting for transfers between devices, on_device(): code_grad = lax.psum(code_parts, ('layer', 'latent'))  65.5 us
    unnamed x12, local copies, waits for them, and re-layouts  59.9 us
    dot_general x4, matrix products, contract_cols(): lax.dot_general(left, right, (((1,), (1,)), ((), ())), preferred_element_...  27.6 us
    while x1, local copies, waits for them, and re-layouts, on_device(): partials = lax.fori_loop(source, stop_at, forward_step, partials)  25.9 us
    dot_general x4, matrix products, contract_rows(): lax.dot_general(left, right, (((0,), (0,)), ((), ())), preferred_element_...  24.6 us
    dot_general x4, matrix products, forward_step(): jnp.dot(dense_codes, weight_slab, preferred_element_type=jnp.float32)  20.9 us
    broadcast_in_dim x1, local copies, waits for them, and re-layouts, on_device(): jnp.zeros(decoder.shape, jnp.bfloat16)  12.5 us
  transfers between devices with their start and end apart: 3, of which 3 were waited for; matrix products, arithmetic and copies ran while one was open for 11% of the time, Pallas kernels for 0%

profile of v1, /device:TPU:0, one launch (start us, length us, event | category | flops | bytes accessed | tf_op | source)
XLA Modules:
  0.0 545.9 jit_solution(17231205610036496668)
XLA Ops:
  7.2 25.9 %copy.19 = bf16[2048,4,2304]{2,0,1:T(8,128)(2,1)} copy(bf16[2048,4,2304]{2,1,0:T(4,128)(2,1)} %param.9) | data formatting | bytes 75497472 | tf_op jit(solution)/shard_map/while | solution.py:57
  33.1 0.7 bitcast_convert_fusion
  34.1 9.8 %fusion.21 = bf16[128,2048]{1,0:T(8,128)(2,1)S(1)} fusion(f32[128,64]{1,0:T(8,128)S(1)} %copy.18, s32[2048]{0:T(1024)S(1)} %iota_add_fusion, s32[128,64]{1,0:T(8,128)S(1)} %copy.17), kind=kLoop, calls=%fused_computation.21 | loop fusion | flops 50069504 | bytes 598016 | tf_op jit(solution)/shard_map/reduce_sum | solution.py:19
  43.9 2.6 broadcast_in_dim.51.clone
  46.5 26.9 %while.22 = (s32[]{:T(128)}, f32[4,128,2304]{2,1,0:T(8,128)}, bf16[2048,4,2304]{2,0,1:T(8,128)(2,1)}, bf16[128,2048]{1,0:T(8,128)(2,1)S(1)}, s32[]{:T(128)}, /*index=5*/s32[]{:T(128)}, s32[]{:T(128)}) while((s32[]{:T(128)}, f32[4,128,2304]{2,1,0:T(8,128)}, bf16[2048,4,2304]{2,0,1:T(8,128)(2,1)}, bf16[128,2048]{1,0:T(8,128)(2,1)S(1)}, ...), condition=%wide.region_2.3_spmd, body=%wide.region_1.2_spmd.sunk | while | flops 1207959552 | bytes 15859839 | solution.py:57
  46.5 5.2 fusion.37
  52.1 1.1 constant_dynamic-update-slice_fusion.3
  53.2 5.2 fusion.37
  58.8 1.1 constant_dynamic-update-slice_fusion.3
  59.9 5.2 fusion.37
  65.5 1.1 constant_dynamic-update-slice_fusion.3
  66.6 5.2 fusion.37
  72.2 1.2 constant_dynamic-update-slice_fusion.3
  73.5 172.9 %all-reduce.4.cloned.1.call-done = f32[4,128,2304]{2,1,0:T(8,128)} async-done(((f32[4,128,2304]{2,1,0:T(8,128)}), f32[4,128,2304]{2,1,0:T(8,128)}) %all-reduce.4.cloned.1.call-update) | async-done | bytes 4718608 | tf_op jit(solution)/shard_map/psum | solution.py:13
  246.4 88.8 %all-reduce.6.cloned.1.call-done = f32[4,128,2304]{2,1,0:T(8,128)} async-done(((f32[4,128,2304]{2,1,0:T(8,128)}), f32[4,128,2304]{2,1,0:T(8,128)}) %all-reduce.6.cloned.1.call-update) | async-done | bytes 4718608 | tf_op jit(solution)/shard_map/psum | solution.py:13
  335.3 4.1 fusion.23
  339.4 12.5 %broadcast_in_dim.54 = bf16[2048,4,2304]{0,2,1:T(8,128)(2,1)} broadcast(bf16[]{:T(256)} %constant.88.clone.1), dimensions={} | broadcast | bytes 37748736 | tf_op jit(solution)/shard_map/broadcast_in_dim | solution.py:72
  352.0 52.3 %while.23 = (s32[]{:T(128)}, bf16[2048,4,2304]{0,2,1:T(8,128)(2,1)}, f32[128,2048]{1,0:T(8,128)S(1)}, bf16[4,128,2304]{2,1,0:T(8,128)(2,1)S(1)}, bf16[128,2048]{...) while((s32[]{:T(128)}, bf16[2048,4,2304]{0,2,1:T(8,128)(2,1)}, ...), condition=%wide.region_7.8_spmd, body=%wide.region_6.7_spmd.sunk | while | flops 2420899840 | bytes 22677640 | solution.py:75
  352.0 6.1 %fusion.42 = bf16[2048,4,2304]{0,2,1:T(8,128)(2,1)} fusion(bf16[2048,4,2304]{0,2,1:T(8,128)(2,1)} %get-tuple-element.205, s32[]{:T(128)S(6)} %select_n.54, bf16[128,2048]{1,0:T(8,128)(2,1)} %get-tuple-element.217, bf16[4,128,2304]{2,1,0:T(8,128)(2,1)S(1)} %get-tuple-element.216), kind=kOutput, calls=%fused_computation.8.clone.1 | convolution fusion | flops 1212678144 | bytes 10552320 | tf_op jit(solution)/shard_map/while/body/dot_general | solution.py:24
  358.2 6.9 %fusion.43 = f32[128,2048]{1,0:T(8,128)S(1)} fusion(f32[128,2048]{1,0:T(8,128)S(1)} %get-tuple-element.206, bf16[2048,4,2304]{2,0,1:T(8,128)(2,1)} %get-tuple-element.218, s32[]{:T(128)S(6)} %select_n.54, bf16[4,128,2304]{2,1,0:T(8,128)(2,1)S(1)} %get-tuple-element.216), kind=kOutput, calls=%fused_computation.12.clone.1 | convolution fusion | flops 1208221696 | bytes 12125184 | tf_op jit(solution)/shard_map/while/body/dot_general | solution.py:30
  365.1 6.1 %fusion.42 = bf16[2048,4,2304]{0,2,1:T(8,128)(2,1)} fusion(bf16[2048,4,2304]{0,2,1:T(8,128)(2,1)} %get-tuple-element.205, s32[]{:T(128)S(6)} %select_n.54, bf16[128,2048]{1,0:T(8,128)(2,1)} %get-tuple-element.217, bf16[4,128,2304]{2,1,0:T(8,128)(2,1)S(1)} %get-tuple-element.216), kind=kOutput, calls=%fused_computation.8.clone.1 | convolution fusion | flops 1212678144 | bytes 10552320 | tf_op jit(solution)/shard_map/while/body/dot_general | solution.py:24
  371.2 6.9 %fusion.43 = f32[128,2048]{1,0:T(8,128)S(1)} fusion(f32[128,2048]{1,0:T(8,128)S(1)} %get-tuple-element.206, bf16[2048,4,2304]{2,0,1:T(8,128)(2,1)} %get-tuple-element.218, s32[]{:T(128)S(6)} %select_n.54, bf16[4,128,2304]{2,1,0:T(8,128)(2,1)S(1)} %get-tuple-element.216), kind=kOutput, calls=%fused_computation.12.clone.1 | convolution fusion | flops 1208221696 | bytes 12125184 | tf_op jit(solution)/shard_map/while/body/dot_general | solution.py:30
  378.1 6.2 %fusion.42 = bf16[2048,4,2304]{0,2,1:T(8,128)(2,1)} fusion(bf16[2048,4,2304]{0,2,1:T(8,128)(2,1)} %get-tuple-element.205, s32[]{:T(128)S(6)} %select_n.54, bf16[128,2048]{1,0:T(8,128)(2,1)} %get-tuple-element.217, bf16[4,128,2304]{2,1,0:T(8,128)(2,1)S(1)} %get-tuple-element.216), kind=kOutput, calls=%fused_computation.8.clone.1 | convolution fusion | flops 1212678144 | bytes 10552320 | tf_op jit(solution)/shard_map/while/body/dot_general | solution.py:24
  384.3 6.9 %fusion.43 = f32[128,2048]{1,0:T(8,128)S(1)} fusion(f32[128,2048]{1,0:T(8,128)S(1)} %get-tuple-element.206, bf16[2048,4,2304]{2,0,1:T(8,128)(2,1)} %get-tuple-element.218, s32[]{:T(128)S(6)} %select_n.54, bf16[4,128,2304]{2,1,0:T(8,128)(2,1)S(1)} %get-tuple-element.216), kind=kOutput, calls=%fused_computation.12.clone.1 | convolution fusion | flops 1208221696 | bytes 12125184 | tf_op jit(solution)/shard_map/while/body/dot_general | solution.py:30
  391.2 6.1 %fusion.42 = bf16[2048,4,2304]{0,2,1:T(8,128)(2,1)} fusion(bf16[2048,4,2304]{0,2,1:T(8,128)(2,1)} %get-tuple-element.205, s32[]{:T(128)S(6)} %select_n.54, bf16[128,2048]{1,0:T(8,128)(2,1)} %get-tuple-element.217, bf16[4,128,2304]{2,1,0:T(8,128)(2,1)S(1)} %get-tuple-element.216), kind=kOutput, calls=%fused_computation.8.clone.1 | convolution fusion | flops 1212678144 | bytes 10552320 | tf_op jit(solution)/shard_map/while/body/dot_general | solution.py:24
  397.4 6.9 %fusion.43 = f32[128,2048]{1,0:T(8,128)S(1)} fusion(f32[128,2048]{1,0:T(8,128)S(1)} %get-tuple-element.206, bf16[2048,4,2304]{2,0,1:T(8,128)(2,1)} %get-tuple-element.218, s32[]{:T(128)S(6)} %select_n.54, bf16[4,128,2304]{2,1,0:T(8,128)(2,1)S(1)} %get-tuple-element.216), kind=kOutput, calls=%fused_computation.12.clone.1 | convolution fusion | flops 1208221696 | bytes 12125184 | tf_op jit(solution)/shard_map/while/body/dot_general | solution.py:30
  404.3 9.0 %fusion.22 = f32[128,64]{1,0:T(8,128)S(1)} fusion(f32[128,2048]{1,0:T(8,128)S(1)} %get-tuple-element.60, s32[2048]{0:T(1024)S(1)} %iota_add_fusion, s32[128,64]{1,0:T(8,128)S(1)} %copy.17), kind=kLoop, calls=%fused_computation.22 | loop fusion | flops 50323456 | bytes 1122304 | tf_op jit(solution)/shard_map/reduce_sum | solution.py:76
  413.4 0.6 copy-done.3
  414.1 0.5 broadcast_multiply_fusion
  414.6 57.6 %copy.23 = bf16[2048,4,2304]{2,1,0:T(4,128)(2,1)} copy(bf16[2048,4,2304]{0,2,1:T(8,128)(2,1)} %get-tuple-element.88) | data formatting | bytes 75497472
  472.2 65.5 %all-reduce.8.cloned.1.call-done = f32[4,128,64]{1,2,0:T(8,128)} async-done(((f32[4,128,64]{1,2,0:T(8,128)}), f32[4,128,64]{1,2,0:T(8,128)}) %all-reduce.8.cloned.1.call-update) | async-done | bytes 131088 | tf_op jit(solution)/shard_map/psum | solution.py:80
  537.8 1.6 copy.52
  (27 shorter events, 2.1 us)
Async XLA Ops:
  7.2 26.8 %copy-start = (s32[4,128,64]{1,2,0:T(8,128)S(1)}, s32[4,128,64]{1,2,0:T(8,128)}, u32[]{:S(2)}) copy-start(s32[4,128,64]{1,2,0:T(8,128)} %param.10) | copy-start | bytes 393220
  7.2 239.2 %all-reduce.4.cloned.1.call-start = ((), (), s32[]{:S(2)}) async-start(), calls=%async_computation | async-start | bytes 9437184 | tf_op jit(solution)/shard_map/psum | solution.py:13
  73.4 266.0 %copy-start.2 = (bf16[128,2048]{1,0:T(8,128)(2,1)}, bf16[128,2048]{1,0:T(8,128)(2,1)S(1)}, u32[]{:S(2)}) copy-start(bf16[128,2048]{1,0:T(8,128)(2,1)S(1)} %get-tuple-element.231) | copy-start | bytes 1572868
  73.4 261.9 %copy-start.4 = (f32[4,2304]{1,0:T(4,128)S(1)}, f32[4,2304]{1,0:T(4,128)}, u32[]{:S(2)}) copy-start(f32[4,2304]{1,0:T(4,128)} %param.12) | copy-start | bytes 110596
  73.4 261.8 %all-reduce.6.cloned.1.call-start = ((), (), s32[]{:S(2)}) async-start(), calls=%async_computation.1 | async-start | bytes 9437184 | tf_op jit(solution)/shard_map/psum | solution.py:13
  246.4 291.4 %all-reduce.8.cloned.1.call-start = ((), (), s32[]{:S(2)}) async-start(), calls=%async_computation.2 | async-start | bytes 262144 | tf_op jit(solution)/shard_map/psum | solution.py:80
  413.4 0.7 copy-start.3
  414.6 124.7 %copy-start.1 = (s32[4,128,64]{1,2,0:T(8,128)S(1)}, s32[4,128,64]{1,2,0:T(8,128)}, u32[]{:S(2)}) copy-start(s32[4,128,64]{1,2,0:T(8,128)} %param.10) | copy-start | bytes 393220
Sparse Core Ops, SparseCore 0:
  73.5 172.7 all-reduce.3
  249.7 85.5 all-reduce.5
  414.2 123.4 all-reduce.7
